TPU v7x, 32 devices: a whole 2x2x4 slice. The times are simulated.
32 devices in a mesh: dp: 8 (over z, x), expert: 4 (over y, core).
Axes of the slice: x: 2, y: 2, z: 4, core: 2. Of those that a mesh axis runs over, the one named last changes fastest.
Arguments:
- tokens: bfloat16 [32768, 768], P(('dp', 'expert')), may hold values from -6 to 6
- prev_scores: float32 [32768, 8], P(('dp', 'expert')), may hold values from -6 to 6
- segments: int32 [32, 1024], P(('dp', 'expert')), may hold values from 0 to 7, never falling along the last dimension, each value on 1 to 512 neighbouring positions
- routes: int32 [32768, 2], P(('dp', 'expert')), may hold values from 0 to 7, all different within a row; in each aligned block of 1024 rows (0 to 1023, 1024 to 2047, ...) at most 256 rows name the same one
- wqkv: bfloat16 [768, 2304], P('dp'), may hold values from -0.21875 to 0.21875
- wo: bfloat16 [768, 768], P('dp'), may hold values from -1.75 to 1.75
- router: bfloat16 [768, 8], P('dp'), may hold values from -0.125 to 0.125
- const_gate: bfloat16 [768, 4], P('dp'), may hold values from -0.21875 to 0.21875
- const_vec: bfloat16 [768, 2], P('dp'), may hold values from -5 to 5
- gain1: bfloat16 [768], P('dp'), may hold values from 0.5 to 1.5
- gain2: bfloat16 [768], P('dp'), may hold values from 0.5 to 1.5
- gate_mix: bfloat16 [8, 8], replicated, may hold values from -0.8984375 to 0.8984375
- w_in: bfloat16 [4, 768, 4096], P('expert'), may hold values from -0.21875 to 0.21875
- w_out: bfloat16 [4, 2048, 768], P('expert'), may hold values from -0.125 to 0.125
- cotangent: bfloat16 [32768, 768], P(('dp', 'expert')), may hold values from -6 to 6
Outputs:
- mixed: bfloat16 [32768, 768], P(('dp', 'expert'))
- grad_tokens: float32 [32768, 768], P(('dp', 'expert'))
- grad_prev: float32 [32768, 8], P(('dp', 'expert'))
- grad_wqkv: float32 [768, 2304], P('dp')
- grad_wo: float32 [768, 768], P('dp')
- grad_router: float32 [768, 8], P('dp')
- grad_const_gate: float32 [768, 4], P('dp')
- grad_const_vec: float32 [768, 2], P('dp')
- grad_gain1: float32 [768], P('dp')
- grad_gain2: float32 [768], P('dp')
- grad_gate_mix: float32 [8, 8], replicated
- grad_w_in: float32 [4, 768, 4096], P('expert', 'dp')
- grad_w_out: float32 [4, 2048, 768], P('expert', 'dp')
Inputs may be any that keep to these rules, and one draw needn't show every extreme that they name: `routes`: each token names two different experts. Within the tokens of one device (aligned blocks of 1024 rows), no expert is named by more than 256 tokens, and some expert reaches 256. `segments`: within a sequence the numbers never fall; a document has at most 512 positions, and one has exactly that many.
All inputs are finite; a program needn't handle non-finite values.
Results may differ from a plain program's by a relative error of at most 0.014.
The roundings to bfloat16 on the way count: a program that leaves them out, or rounds other values in their place, can miss the bound.
Values may be sent and summed in bfloat16 or wider, within the bound.
A program may use at most 256 MiB of HBM per device.

v0:
```python
import jax
import jax.numpy as jnp
from jax import lax
from jax.sharding import PartitionSpec as P

HEADS = 12
HEAD_DIM = 64
CAP = 256


NORM_EPSILON = 1e-06
HIGHEST_PRECISION = lax.Precision.HIGHEST
NEGATIVE = -1e30


def rotate(values, cosines, sine_table):
    half_width = values.shape[-1] // 2
    front_half = values[..., :half_width]
    back_half = values[..., half_width:]
    return jnp.concatenate(
        [
            front_half * cosines - back_half * sine_table,
            back_half * cosines + front_half * sine_table,
        ],
        axis=-1,
    )


def pair_softmax(picked):
    weights = jnp.exp(picked - jnp.max(picked, axis=-1, keepdims=True))
    return weights / jnp.sum(weights, axis=-1, keepdims=True)


def pair_softmax_back(weights, upstream):
    return weights * (upstream - jnp.sum(weights * upstream, axis=-1, keepdims=True))


def norm_back(upstream, normed, inverse):
    return inverse * (upstream - normed * jnp.mean(upstream * normed, axis=-1, keepdims=True))


def masked_scores(q_block, key_rows, seg_rows, seg_keys, row_start):
    scores = jnp.einsum("qhd,khd->hqk", q_block, key_rows, preferred_element_type=jnp.float32)
    row_ids = row_start + jnp.arange(q_block.shape[0], dtype=jnp.int32)
    col_ids = jnp.arange(key_rows.shape[0], dtype=jnp.int32)
    allowed = (col_ids[None, :] <= row_ids[:, None]) & (seg_rows[:, None] == seg_keys[None, :])
    return jnp.where(allowed[None], scores, NEGATIVE)


def per_device(
    tokens,
    prev_scores,
    segments,
    routes,
    wqkv,
    wo,
    router,
    const_gate,
    const_vec,
    gain1,
    gain2,
    gate_mix,
    w_in,
    w_out,
    cotangent,
):
    wqkv_full, wo_full, router_full, cgate_full, cvec_full, gain_attn, gain_ffn = (
        lax.all_gather(wqkv, "dp", axis=0, tiled=True),
        lax.all_gather(wo, "dp", axis=0, tiled=True),
        lax.all_gather(router, "dp", axis=0, tiled=True),
        lax.all_gather(const_gate, "dp", axis=0, tiled=True),
        lax.all_gather(const_vec, "dp", axis=0, tiled=True),
        lax.all_gather(gain1, "dp", axis=0, tiled=True),
        lax.all_gather(gain2, "dp", axis=0, tiled=True),
    )
    tok_count, model_width = tokens.shape
    seq_count, seq_len = segments.shape
    head_count = HEADS
    head_size = HEAD_DIM
    kind_count = router.shape[1]
    experts = w_in.shape[0] * lax.axis_size("expert")
    hidden_width = w_out.shape[1]
    capacity = CAP
    scale = head_size ** (-0.5)
    resid_in = tokens.astype(jnp.float32)
    inverse_one = lax.rsqrt(jnp.mean(resid_in * resid_in, axis=-1, keepdims=True) + NORM_EPSILON)
    normed_one = resid_in * inverse_one
    gain_one = gain_attn.astype(jnp.float32)
    attn_in = (normed_one * gain_one).astype(jnp.bfloat16)
    qkv_proj = jnp.dot(attn_in, wqkv_full, preferred_element_type=jnp.float32).reshape(
        tok_count, 3, head_count, head_size
    )
    positions = (jnp.arange(tok_count, dtype=jnp.int32) % seq_len).astype(jnp.float32)
    frequency = 10000.0 ** (-jnp.arange(head_size // 2).astype(jnp.float32) / (head_size // 2))
    angles = positions[:, None, None] * frequency[None, None, :]
    cosines = jnp.cos(angles)
    sine_table = jnp.sin(angles)
    queries = (rotate(qkv_proj[:, 0], cosines, sine_table) * scale).astype(jnp.bfloat16)
    key_rows = rotate(qkv_proj[:, 1], cosines, sine_table).astype(jnp.bfloat16)
    value_rows = qkv_proj[:, 2].astype(jnp.bfloat16)
    seq_shape = (seq_count, seq_len, head_count, head_size)
    query_seqs = queries.reshape(seq_shape)
    key_seqs = key_rows.reshape(seq_shape)
    value_seqs = value_rows.reshape(seq_shape)
    block_rows = min(512, seq_len)
    per_seq = seq_len // block_rows
    block_count = seq_count * per_seq

    def block_inputs(block_index):
        seq_index = block_index // per_seq
        row_start = block_index % per_seq * block_rows
        seg_keys = segments[seq_index]
        q_block = lax.dynamic_slice_in_dim(query_seqs[seq_index], row_start, block_rows, 0)
        seg_rows = lax.dynamic_slice_in_dim(seg_keys, row_start, block_rows, 0)
        scores = masked_scores(q_block, key_seqs[seq_index], seg_rows, seg_keys, row_start)
        return (seq_index, row_start, q_block, scores)

    def forward_block(block_index):
        seq_index, row_start, q_block, scores = block_inputs(block_index)
        row_max = jnp.max(scores, axis=-1, keepdims=True)
        expd = jnp.exp(scores - row_max)
        row_total = jnp.sum(expd, axis=-1, keepdims=True)
        prob_rows = (expd / row_total).astype(jnp.bfloat16)
        attended = jnp.einsum(
            "hqk,khd->qhd", prob_rows, value_seqs[seq_index], preferred_element_type=jnp.float32
        )
        return (attended, row_max + jnp.log(row_total))

    attended, log_totals = lax.map(forward_block, jnp.arange(block_count, dtype=jnp.int32))
    attn_out = attended.reshape(tok_count, model_width).astype(jnp.bfloat16)
    resid_mid = resid_in + jnp.dot(attn_out, wo_full, preferred_element_type=jnp.float32)
    inverse_two = lax.rsqrt(jnp.mean(resid_mid * resid_mid, axis=-1, keepdims=True) + NORM_EPSILON)
    normed_two = resid_mid * inverse_two
    gain_two = gain_ffn.astype(jnp.float32)
    ffn_norm = normed_two * gain_two
    ffn_in = ffn_norm.astype(jnp.bfloat16)
    mix_matrix = gate_mix.astype(jnp.float32)
    logits = jnp.dot(ffn_in, router_full, preferred_element_type=jnp.float32) + jnp.dot(
        prev_scores, mix_matrix, precision=HIGHEST_PRECISION
    )
    route_hot = (
        routes[:, :, None] == jnp.arange(kind_count, dtype=jnp.int32)[None, None, :]
    ).astype(jnp.float32)
    gates = pair_softmax(jnp.sum(logits[:, None, :] * route_hot, axis=-1))
    mix_logits = jnp.dot(ffn_in, cgate_full, preferred_element_type=jnp.float32)
    alpha_one = pair_softmax(mix_logits[:, 0:2])
    alpha_two = pair_softmax(mix_logits[:, 2:4])
    const_values = cvec_full.astype(jnp.float32)
    const_one = alpha_one[:, 0:1] * ffn_norm + alpha_one[:, 1:2] * const_values[:, 0][None, :]
    const_two = alpha_two[:, 0:1] * ffn_norm + alpha_two[:, 1:2] * const_values[:, 1][None, :]
    flat_routes = routes.reshape(-1)
    assign_count = flat_routes.shape[0]
    route_onehot = (
        flat_routes[:, None] == jnp.arange(kind_count, dtype=jnp.int32)[None, :]
    ).astype(jnp.int32)
    earlier = jnp.cumsum(route_onehot, axis=0) - route_onehot
    slot_ids = jnp.sum(earlier * route_onehot, axis=1)
    target = jnp.where(flat_routes < experts, flat_routes * capacity + slot_ids, experts * capacity)
    slot_owner = jnp.full((experts * capacity,), assign_count, jnp.int32)
    slot_owner = slot_owner.at[target].set(jnp.arange(assign_count, dtype=jnp.int32), mode="drop")
    owner_token = jnp.where(slot_owner == assign_count, tok_count, slot_owner // 2)
    ffn_padded = jnp.concatenate([ffn_in, jnp.zeros((1, model_width), jnp.bfloat16)], axis=0)
    send_rows = ffn_padded[owner_token].reshape(experts, capacity, model_width)
    recv_rows = lax.all_to_all(send_rows, "expert", split_axis=0, concat_axis=1, tiled=True)
    gate_up = jnp.einsum("erd,edf->erf", recv_rows, w_in, preferred_element_type=jnp.float32)
    gate_part = gate_up[..., :hidden_width]
    up_part = gate_up[..., hidden_width:]
    sigmoid_gate = jax.nn.sigmoid(gate_part)
    hidden_act = (gate_part * sigmoid_gate * up_part).astype(jnp.bfloat16)
    expert_out = jnp.einsum(
        "erf,efd->erd", hidden_act, w_out, preferred_element_type=jnp.float32
    ).astype(jnp.bfloat16)
    returned = lax.all_to_all(expert_out, "expert", split_axis=1, concat_axis=0, tiled=True)
    out_padded = jnp.concatenate(
        [
            returned.reshape(experts * capacity, model_width),
            jnp.zeros((1, model_width), jnp.bfloat16),
        ],
        axis=0,
    )
    ffn_rows = out_padded[target].astype(jnp.float32).reshape(tok_count, 2, model_width)
    is_ffn = (routes < experts).astype(jnp.float32)
    is_copy = (routes == experts + 1).astype(jnp.float32)
    is_one = (routes == experts + 2).astype(jnp.float32)
    is_two = (routes == experts + 3).astype(jnp.float32)
    branch = (
        ffn_rows * is_ffn[:, :, None]
        + ffn_norm[:, None, :] * is_copy[:, :, None]
        + const_one[:, None, :] * is_one[:, :, None]
        + const_two[:, None, :] * is_two[:, :, None]
    )
    mixed = (resid_mid + jnp.sum(gates[:, :, None] * branch, axis=1)).astype(jnp.bfloat16)
    upstream = cotangent.astype(jnp.float32)
    gate_grad = jnp.sum(branch * upstream[:, None, :], axis=-1)
    weighted = (
        (gates[:, :, None] * upstream[:, None, :])
        .reshape(assign_count, model_width)
        .astype(jnp.bfloat16)
    )
    weighted_padded = jnp.concatenate([weighted, jnp.zeros((1, model_width), jnp.bfloat16)], axis=0)
    slot_grads = weighted_padded[slot_owner].reshape(experts, capacity, model_width)
    grad_sent = lax.all_to_all(slot_grads, "expert", split_axis=0, concat_axis=1, tiled=True)
    hidden_grad = jnp.einsum("erd,efd->erf", grad_sent, w_out, preferred_element_type=jnp.float32)
    gate_grad_h = hidden_grad * up_part * sigmoid_gate * (1.0 + gate_part * (1.0 - sigmoid_gate))
    up_grad = hidden_grad * gate_part * sigmoid_gate
    front_grad = jnp.concatenate([gate_grad_h, up_grad], axis=-1).astype(jnp.bfloat16)
    rows_grad = jnp.einsum(
        "erf,edf->erd", front_grad, w_in, preferred_element_type=jnp.float32
    ).astype(jnp.bfloat16)
    back_rows = lax.all_to_all(rows_grad, "expert", split_axis=1, concat_axis=0, tiled=True)
    back_padded = jnp.concatenate(
        [
            back_rows.reshape(experts * capacity, model_width),
            jnp.zeros((1, model_width), jnp.bfloat16),
        ],
        axis=0,
    )
    ffn_in_grad = jnp.sum(
        back_padded[target].astype(jnp.float32).reshape(tok_count, 2, model_width), axis=1
    )
    weight_one = jnp.sum(gates * is_one, axis=1)
    weight_two = jnp.sum(gates * is_two, axis=1)
    weight_copy = jnp.sum(gates * is_copy, axis=1)
    dot_norm = jnp.sum(upstream * ffn_norm, axis=-1)
    dot_vecs = jnp.dot(cotangent, cvec_full, preferred_element_type=jnp.float32)
    alpha_grad_one = weight_one[:, None] * jnp.stack([dot_norm, dot_vecs[:, 0]], axis=1)
    alpha_grad_two = weight_two[:, None] * jnp.stack([dot_norm, dot_vecs[:, 1]], axis=1)
    mix_grad = jnp.concatenate(
        [
            pair_softmax_back(alpha_one, alpha_grad_one),
            pair_softmax_back(alpha_two, alpha_grad_two),
        ],
        axis=1,
    ).astype(jnp.bfloat16)
    grad_cgate = jnp.einsum("td,tk->dk", ffn_in, mix_grad, preferred_element_type=jnp.float32)
    vec_weights = jnp.stack([weight_one * alpha_one[:, 1], weight_two * alpha_two[:, 1]], axis=1)
    grad_cvec = jnp.einsum("td,tk->dk", upstream, vec_weights, precision=HIGHEST_PRECISION)
    picked_grad = pair_softmax_back(gates, gate_grad)
    logit_grad = jnp.sum(route_hot * picked_grad[:, :, None], axis=1).astype(jnp.bfloat16)
    grad_router = jnp.einsum("td,tk->dk", ffn_in, logit_grad, preferred_element_type=jnp.float32)
    logit_wide = logit_grad.astype(jnp.float32)
    grad_mix = jnp.einsum("tk,tj->kj", prev_scores, logit_wide, precision=HIGHEST_PRECISION)
    grad_prev = jnp.einsum("tj,kj->tk", logit_grad, gate_mix, preferred_element_type=jnp.float32)
    norm_grad_two = (
        ffn_in_grad
        + jnp.einsum("tk,dk->td", logit_grad, router_full, preferred_element_type=jnp.float32)
        + jnp.einsum("tk,dk->td", mix_grad, cgate_full, preferred_element_type=jnp.float32)
        + (weight_copy + weight_one * alpha_one[:, 0] + weight_two * alpha_two[:, 0])[:, None]
        * upstream
    )
    grad_gain2 = jnp.sum(norm_grad_two * normed_two, axis=0)
    mid_grad = upstream + norm_back(norm_grad_two * gain_two, normed_two, inverse_two)
    proj_grad = mid_grad.astype(jnp.bfloat16)
    grad_wo = jnp.einsum("td,te->de", attn_out, proj_grad, preferred_element_type=jnp.float32)
    attn_grad = jnp.einsum(
        "te,de->td", proj_grad, wo_full, preferred_element_type=jnp.float32
    ).astype(jnp.bfloat16)
    attn_grad_seqs = attn_grad.reshape(seq_shape)

    def backward_block(packed):
        block_index, log_total = packed
        seq_index, row_start, q_block, scores = block_inputs(block_index)
        prob_rows = jnp.exp(scores - log_total)
        out_grad_block = lax.dynamic_slice_in_dim(
            attn_grad_seqs[seq_index], row_start, block_rows, 0
        )
        prob_grad = jnp.einsum(
            "qhd,khd->hqk",
            out_grad_block,
            value_seqs[seq_index],
            preferred_element_type=jnp.float32,
        )
        row_delta = jnp.sum(prob_rows * prob_grad, axis=-1, keepdims=True)
        score_grad = (prob_rows * (prob_grad - row_delta)).astype(jnp.bfloat16)
        query_grad = jnp.einsum(
            "hqk,khd->qhd", score_grad, key_seqs[seq_index], preferred_element_type=jnp.float32
        )
        key_grad = jnp.einsum(
            "hqk,qhd->khd", score_grad, q_block, preferred_element_type=jnp.float32
        )
        value_grad = jnp.einsum(
            "hqk,qhd->khd",
            prob_rows.astype(jnp.bfloat16),
            out_grad_block,
            preferred_element_type=jnp.float32,
        )
        return (query_grad, key_grad, value_grad)

    query_grad, key_grad, value_grad = lax.map(
        backward_block, (jnp.arange(block_count, dtype=jnp.int32), log_totals)
    )
    query_grad = query_grad.reshape(tok_count, head_count, head_size)
    key_grad = jnp.sum(
        key_grad.reshape(seq_count, per_seq, seq_len, head_count, head_size), axis=1
    ).reshape(tok_count, head_count, head_size)
    value_grad = jnp.sum(
        value_grad.reshape(seq_count, per_seq, seq_len, head_count, head_size), axis=1
    ).reshape(tok_count, head_count, head_size)
    query_back = rotate(query_grad * scale, cosines, -sine_table)
    key_back = rotate(key_grad, cosines, -sine_table)
    qkv_grad = (
        jnp.stack([query_back, key_back, value_grad], axis=1)
        .reshape(tok_count, 3 * model_width)
        .astype(jnp.bfloat16)
    )
    grad_wqkv = jnp.einsum("td,tf->df", attn_in, qkv_grad, preferred_element_type=jnp.float32)
    attn_in_grad = jnp.einsum("tf,df->td", qkv_grad, wqkv_full, preferred_element_type=jnp.float32)
    grad_gain1 = jnp.sum(attn_in_grad * normed_one, axis=0)
    grad_tokens = mid_grad + norm_back(attn_in_grad * gain_one, normed_one, inverse_one)
    summed = lax.psum(
        (grad_wqkv, grad_wo, grad_router, grad_cgate, grad_cvec, grad_gain1, grad_gain2), "expert"
    )
    shares = (
        lax.psum_scatter(summed[0], "dp", scatter_dimension=0, tiled=True),
        lax.psum_scatter(summed[1], "dp", scatter_dimension=0, tiled=True),
        lax.psum_scatter(summed[2], "dp", scatter_dimension=0, tiled=True),
        lax.psum_scatter(summed[3], "dp", scatter_dimension=0, tiled=True),
        lax.psum_scatter(summed[4], "dp", scatter_dimension=0, tiled=True),
        lax.psum_scatter(summed[5], "dp", scatter_dimension=0, tiled=True),
        lax.psum_scatter(summed[6], "dp", scatter_dimension=0, tiled=True),
    )
    grad_gate_mix = lax.psum(grad_mix, ("dp", "expert"))
    grad_w_in = jnp.einsum(
        "erd,erf->edf", recv_rows, front_grad, preferred_element_type=jnp.float32
    )
    grad_w_out = jnp.einsum(
        "erf,erd->efd", hidden_act, grad_sent, preferred_element_type=jnp.float32
    )
    expert_shares = (
        lax.psum_scatter(grad_w_in, "dp", scatter_dimension=1, tiled=True),
        lax.psum_scatter(grad_w_out, "dp", scatter_dimension=1, tiled=True),
    )
    in_share = expert_shares[0]
    out_share = expert_shares[1]
    return (
        mixed,
        grad_tokens,
        grad_prev,
        shares[0],
        shares[1],
        shares[2],
        shares[3],
        shares[4],
        shares[5],
        shares[6],
        grad_gate_mix,
        in_share,
        out_share,
    )


def solution(mesh):
    in_specs = (
        P(("dp", "expert"), None),
        P(("dp", "expert"), None),
        P(("dp", "expert"), None),
        P(("dp", "expert"), None),
        P("dp", None),
        P("dp", None),
        P("dp", None),
        P("dp", None),
        P("dp", None),
        P("dp"),
        P("dp"),
        P(),
        P("expert", None, None),
        P("expert", None, None),
        P(("dp", "expert"), None),
    )
    out_specs = (
        P(("dp", "expert"), None),
        P(("dp", "expert"), None),
        P(("dp", "expert"), None),
        P("dp", None),
        P("dp", None),
        P("dp", None),
        P("dp", None),
        P("dp", None),
        P("dp"),
        P("dp"),
        P(),
        P("expert", "dp", None),
        P("expert", "dp", None),
    )
    return jax.shard_map(
        per_device, mesh=mesh, in_specs=in_specs, out_specs=out_specs, check_vma=False
    )
```

profile of v0, /device:TPU:0, one launch (start us, length us, event | category | flops | bytes accessed | tf_op | source)
XLA Modules:
  0.0 1413.7 jit_solution(5160941601331199493)
XLA Ops:
  15.8 22.9 %all-gather.2 = bf16[8,96,2]{1,2,0:T(2,128)(2,1)S(1)} all-gather(bf16[1,96,2]{1,2,0:T(2,128)(2,1)S(1)} %bitcast.370), channel_id=1, replica_groups=mesh['dp'=8,'expert'=4] {'dp'}, dimensions={0}, use_global_device_ids=true | all-gather | bytes 3456 | tf_op jit(solution)/shard_map/all_gather | solution.py:72
  46.4 18.2 %all-reduce.11 = (bf16[768]{0:T(1024)(128)(2,1)S(1)}, bf16[768]{0:T(1024)(128)(2,1)S(1)}) all-reduce(bf16[768]{0:T(1024)(128)(2,1)S(1)} %dynamic-update-slice, bf16[768]{0:T(1024)(128)(2,1)S(1)} %dynamic-update-slice.1), channel_id=1, replica_groups=mesh['dp'=8,'expert'=4] {'dp'}, use_global_device_ids=true, to_apply=%add.4 | all-reduce | flops 1536 | bytes 6144
  67.7 18.5 %all-gather.1 = bf16[8,96,4]{1,2,0:T(4,128)(2,1)S(1)} all-gather(bf16[1,96,4]{1,2,0:T(4,128)(2,1)S(1)} %bitcast.369), channel_id=1, replica_groups=mesh['dp'=8,'expert'=4] {'dp'}, dimensions={0}, use_global_device_ids=true | all-gather | bytes 6912 | tf_op jit(solution)/shard_map/all_gather | solution.py:71
  86.9 26.3 %all-gather = bf16[8,96,8]{1,2,0:T(8,128)(2,1)S(1)} all-gather(bf16[1,96,8]{1,2,0:T(8,128)(2,1)S(1)} %bitcast.368), channel_id=1, replica_groups=mesh['dp'=8,'expert'=4] {'dp'}, dimensions={0}, use_global_device_ids=true | all-gather | bytes 13824 | tf_op jit(solution)/shard_map/all_gather | solution.py:70
  121.6 8.4 scatter_custom_fusion
  139.8 8.5 mul.725
  163.4 82.9 %while.32 = (s32[]{:T(128)}, bf16[2,512,12,64]{1,3,2,0:T(8,128)(2,1)}, f32[2,12,512,1]{2,1,3,0:T(8,128)S(1)}, s32[2]{0:T(128)S(1)}, s32[1,1024]{1,0:T(1,128)S(1)...) while((s32[]{:T(128)}, ...), condition=%wide.region_4.5_spmd.clone, body=%wide.region_1.4_spmd.sunk.clone | while | flops 1668803072 | bytes 102226280 | solution.py:129
  167.1 13.6 select_reduce_fusion.8
  180.7 11.6 fusion.208
  192.4 11.6 bitcast_dynamic-update-slice_fusion.15
  208.2 13.6 select_reduce_fusion.8
  221.8 11.6 fusion.208
  233.5 11.6 bitcast_dynamic-update-slice_fusion.15
  295.5 12.4 convolution_bitcast_fusion
  315.6 12.3 fusion.59
  327.9 12.4 fusion.88
  345.0 12.6 reduce.15
  373.7 11.8 reduce.14
  403.4 10.4 all-to-all-done.1
  418.9 9.4 gather_fusion.3
  429.8 9.5 gather_fusion.1
  439.3 8.0 reshape.775
  447.3 26.8 %multiply_reduce_fusion.1 = (f32[1024,2]{1,0:T(8,128)}, f32[1024,768]{1,0:T(8,128)}) fusion(f32[1024,768]{1,0:T(8,128)} %convert_element_type.252, f32[1024,2]{1,0:T(8,128)} %copy.113, f32[1024,2]{1,0:T(8,128)} %copy.124, f32[1024,768]{1,0:T(8,128)} %get-tuple-element.417, f32[1024,2]{1,0:T(8,128)} %copy.123, f32[1024,768]{1,0:T(8,128)} %get-tuple-element.416, ...), kind=kLoop, calls=%fused_computation.73 | loop fusion | flops 16513024 | bytes 22069248 | tf_op jit(solution)/shard_map/reduce_sum | solution.py:194
  483.4 12.0 reduce_sum.257
  513.3 170.5 %while.33 = (s32[]{:T(128)}, f32[2,512,12,64]{1,3,2,0:T(8,128)}, f32[2,1024,12,64]{1,3,2,0:T(8,128)}, f32[2,1024,12,64]{1,3,2,0:T(8,128)}, s32[2]{0:T(128)S(1)},...) while((s32[]{:T(128)}, f32[2,512,12,64]{1,3,2,0:T(8,128)}, ...), condition=%wide.region_31.32_spmd.clone, body=%wide.region_29.31_spmd.sunk.clone | while | flops 4103596544 | bytes 219347312 | solution.py:289
  516.7 11.8 fusion.217
  528.4 12.9 bitcast_dynamic-update-slice_fusion.19
  541.3 17.5 %multiply_reduce_fusion.12 = (f32[12,512]{1,0:T(8,128)S(1)}, f32[12,512,1024]{2,1,0:T(8,128)}) fusion(f32[12,512,1024]{2,1,0:T(8,128)} %fusion.217, f32[12,512]{1,0:T(8,128)S(1)} %dynamic-slice_bitcast_fusion.3, pred[512,1024]{1,0:T(8,128)(4,1)S(1)} %fusion.218, bf16[1,1024,12,64]{1,3,2,0:T(8,128)(2,1)} %get-tuple-element.687, ...), kind=kOutput, calls=%fused_computation.24.clone.1.clone | convolution fusion | flops 830466048 | bytes 53264388 | tf_op jit(solution)/shard_map/while/body/eval_jaxpr/qhd,khd->hqk/dot_general | solution.py:267
  558.8 21.8 %multiply_convert_fusion.7 = bf16[12,512,1024]{2,1,0:T(8,128)(2,1)} fusion(f32[12,512,1024]{2,1,0:T(8,128)} %get-tuple-element.613, f32[12,512,1024]{2,1,0:T(8,128)} %fusion.217, f32[12,512]{1,0:T(8,128)S(1)} %get-tuple-element.614, f32[12,512]{1,0:T(8,128)S(1)} %dynamic-slice_bitcast_fusion.3, pred[512,1024]{1,0:T(8,128)(4,1)S(1)} %fusion.218), kind=kLoop, calls=%fused_computation.23.clone.1.clone | loop fusion | flops 31457280 | bytes 63488000 | tf_op jit(solution)/shard_map/while/body/eval_jaxpr/convert_element_type | solution.py:274
  580.6 9.8 bitcast_dynamic-update-slice_fusion.17
  590.5 8.5 bitcast_dynamic-update-slice_fusion.18
  602.1 11.4 fusion.217
  613.5 12.6 bitcast_dynamic-update-slice_fusion.19
  626.1 17.4 %multiply_reduce_fusion.12 = (f32[12,512]{1,0:T(8,128)S(1)}, f32[12,512,1024]{2,1,0:T(8,128)}) fusion(f32[12,512,1024]{2,1,0:T(8,128)} %fusion.217, f32[12,512]{1,0:T(8,128)S(1)} %dynamic-slice_bitcast_fusion.3, pred[512,1024]{1,0:T(8,128)(4,1)S(1)} %fusion.218, bf16[1,1024,12,64]{1,3,2,0:T(8,128)(2,1)} %get-tuple-element.687, ...), kind=kOutput, calls=%fused_computation.24.clone.1.clone | convolution fusion | flops 830466048 | bytes 53264388 | tf_op jit(solution)/shard_map/while/body/eval_jaxpr/qhd,khd->hqk/dot_general | solution.py:267
  643.5 21.6 %multiply_convert_fusion.7 = bf16[12,512,1024]{2,1,0:T(8,128)(2,1)} fusion(f32[12,512,1024]{2,1,0:T(8,128)} %get-tuple-element.613, f32[12,512,1024]{2,1,0:T(8,128)} %fusion.217, f32[12,512]{1,0:T(8,128)S(1)} %get-tuple-element.614, f32[12,512]{1,0:T(8,128)S(1)} %dynamic-slice_bitcast_fusion.3, pred[512,1024]{1,0:T(8,128)(4,1)S(1)} %fusion.218), kind=kLoop, calls=%fused_computation.23.clone.1.clone | loop fusion | flops 31457280 | bytes 63488000 | tf_op jit(solution)/shard_map/while/body/eval_jaxpr/convert_element_type | solution.py:274
  665.1 9.8 bitcast_dynamic-update-slice_fusion.17
  674.9 8.6 bitcast_dynamic-update-slice_fusion.18
  716.7 8.8 fusion.60
  725.6 110.9 %reduce-scatter.18.cloned.1.call-done = f32[96,2304]{1,0:T(8,128)} async-done(((f32[768,2304]{1,0:T(8,128)}), f32[96,2304]{1,0:T(8,128)}) %reduce-scatter.18.cloned.1.call-update) | async-done | bytes 884752 | tf_op jit(solution)/shard_map/reduce_scatter | solution.py:314
  836.5 13.4 convolution_bitcast_fusion.1
  850.8 39.6 %psum.63 = f32[8,8]{0,1:T(8,128)S(1)} all-reduce(f32[8,8]{0,1:T(8,128)S(1)} %convolution_bitcast_fusion.3), channel_id=1, replica_groups=mesh['dp'=8,'expert'=4] {'dp','expert'}, use_global_device_ids=true, to_apply=%region_51.52 | all-reduce | flops 64 | bytes 512 | tf_op jit(solution)/shard_map/psum | solution.py:322
  891.0 9.7 fusion.68
  900.7 21.4 %all-reduce.8 = (f32[768]{0:T(1024)S(1)}, f32[768]{0:T(1024)S(1)}) all-reduce(f32[768]{0:T(1024)S(1)} %get-tuple-element.330, f32[768]{0:T(1024)S(1)} %copy-done.57), channel_id=7, replica_groups=mesh['dp'=8,'expert'=4] {'dp'}, use_global_device_ids=true, to_apply=%region_47.48.clone | all-reduce | flops 1536 | bytes 12288
  929.8 35.5 %reduce-scatter.24.cloned.1.call-done = f32[96,4]{1,0:T(8,128)} async-done(((f32[768,4]{1,0:T(8,128)}), f32[96,4]{1,0:T(8,128)}) %reduce-scatter.24.cloned.1.call-update) | async-done | bytes 1552
  966.2 64.3 %reduce-scatter.22.cloned.1.call-done = f32[96,8]{1,0:T(8,128)} async-done(((f32[768,8]{1,0:T(8,128)}), f32[96,8]{1,0:T(8,128)}) %reduce-scatter.22.cloned.1.call-update) | async-done | bytes 3088
  1037.7 114.0 %reduce-scatter.16.cloned.1.call-done = f32[1,256,768]{2,1,0:T(8,128)} async-done(((f32[1,2048,768]{2,1,0:T(8,128)}), f32[1,256,768]{2,1,0:T(8,128)}) %reduce-scatter.16.cloned.1.call-update) | async-done | bytes 786448 | tf_op jit(solution)/shard_map/reduce_scatter | solution.py:331
  1151.7 39.4 %all-reduce.14.cloned.1.call-done = (f32[96,2304]{1,0:T(8,128)}, f32[96,768]{1,0:T(8,128)}) async-done(((f32[96,2304]{1,0:T(8,128)}, f32[96,768]{1,0:T(8,128)}), (f32[96,2304]{1,0:T(8,128)}, f32[96,768]{1,0:T(8,128)})) %all-reduce.14.cloned.1.call-update) | async-done | bytes 1179664 | tf_op jit(solution)/shard_map/psum | solution.py:310
  1191.2 211.6 %reduce-scatter.14.cloned.1.call-done = f32[1,96,4096]{2,1,0:T(8,128)} async-done(((f32[1,768,4096]{2,1,0:T(8,128)}), f32[1,96,4096]{2,1,0:T(8,128)}) %reduce-scatter.14.cloned.1.call-update) | async-done | bytes 1572880 | tf_op jit(solution)/shard_map/reduce_scatter | solution.py:330
  (334 shorter events, 241.1 us)
Async XLA Ops:
  7.2 308.5 %copy-start = (bf16[1,2048,768]{2,1,0:T(8,128)(2,1)S(1)}, bf16[1,2048,768]{2,1,0:T(8,128)(2,1)}, u32[]{:S(2)}) copy-start(bf16[1,2048,768]{2,1,0:T(8,128)(2,1)} %param.32) | copy-start | bytes 9437188
  7.2 8.6 copy-start.63
  7.2 143.1 %all-gather.6.cloned.1.call-start = ((), (), s32[]{:S(2)}) async-start(), calls=%async_computation.11 | async-start | bytes 3981312 | tf_op jit(solution)/shard_map/all_gather | solution.py:68
  7.9 243.0 %all-gather.8.cloned.1.call-start = ((), (), s32[]{:S(2)}) async-start(), calls=%async_computation.12 | async-start | bytes 1327104 | tf_op jit(solution)/shard_map/all_gather | solution.py:69
  39.4 6.5 copy-start.64
  39.4 6.8 copy-start.65
  41.3 26.3 %copy-start.62 = (bf16[96,4]{0,1:T(4,128)(2,1)S(1)}, bf16[96,4]{0,1:T(4,128)(2,1)}, u32[]{:S(2)}) copy-start(bf16[96,4]{0,1:T(4,128)(2,1)} %param.26) | copy-start | bytes 2308
  41.3 45.6 %copy-start.60 = (bf16[96,8]{0,1:T(8,128)(2,1)S(1)}, bf16[96,8]{0,1:T(8,128)(2,1)}, u32[]{:S(2)}) copy-start(bf16[96,8]{0,1:T(8,128)(2,1)} %param.25) | copy-start | bytes 4612
  64.7 85.7 %copy-start.51 = (f32[768]{0:T(1024)}, f32[768]{0:T(1024)S(1)}, u32[]{:S(2)}) copy-start(f32[768]{0:T(1024)S(1)} %convert_element_type.229) | copy-start | bytes 9220
  67.1 83.3 %copy-start.53 = (f32[1024]{0:T(1024)}, f32[1024]{0:T(1024)S(1)}, u32[]{:S(2)}) copy-start(f32[1024]{0:T(1024)S(1)} %add_rsqrt_fusion.1) | copy-start | bytes 12292
  139.8 8.5 copy-start.36
  139.8 8.5 copy-start.58
  150.3 9.2 copy-start.28
  180.7 11.6 copy-start.7
  180.7 11.7 copy-start.20
  221.8 11.6 copy-start.7
  221.8 11.7 copy-start.20
  266.5 6.5 copy-start.34
  266.5 24.7 %all-to-all-start = ((bf16[4,256,768]{2,1,0:T(8,128)(2,1)}), bf16[4,256,768]{2,1,0:T(8,128)(2,1)}, u32[]{:S(2)}, u32[]{:S(2)}) async-start(bf16[4,256,768]{2,1,0:T(8,128)(2,1)} %bitcast.344), calls=%async_computation | async-start | bytes 3145728 | tf_op jit(solution)/shard_map/all_to_all | solution.py:164
  291.2 24.5 %all-to-all-start.2 = ((bf16[4,256,768]{2,1,0:T(8,128)(2,1)}), bf16[4,256,768]{2,1,0:T(8,128)(2,1)}, u32[]{:S(2)}, u32[]{:S(2)}) async-start(bf16[4,256,768]{2,1,0:T(8,128)(2,1)} %bitcast.345), calls=%async_computation.2 | async-start | bytes 3145728 | tf_op jit(solution)/shard_map/all_to_all | solution.py:202
  327.9 12.4 copy-start.66
  327.9 12.4 copy-start.67
  357.5 8.1 copy-start.48
  357.5 8.1 copy-start.47
  361.3 28.1 %all-to-all-start.3 = ((bf16[4,2,98304]{2,1,0:T(2,128)(2,1)}), bf16[4,2,98304]{2,1,0:T(2,128)(2,1)}, u32[]{:S(2)}, u32[]{:S(2)}) async-start(bf16[4,2,98304]{2,1,0:T(2,128)(2,1)} %reshape.850), calls=%async_computation.3 | async-start | bytes 3145728 | tf_op jit(solution)/shard_map/all_to_all | solution.py:210
  385.5 8.2 copy-start.9
  385.5 8.3 copy-start.40
  389.4 24.5 %all-to-all-start.1 = ((bf16[4,2,98304]{2,1,0:T(2,128)(2,1)}), bf16[4,2,98304]{2,1,0:T(2,128)(2,1)}, u32[]{:S(2)}, u32[]{:S(2)}) async-start(bf16[4,2,98304]{2,1,0:T(2,128)(2,1)} %reshape.848), calls=%async_computation.1 | async-start | bytes 3145728 | tf_op jit(solution)/shard_map/all_to_all | solution.py:173
  393.7 331.9 %reduce-scatter.20.cloned.1.call-start = ((), (), s32[]{:S(2)}) async-start(), calls=%async_computation.16 | async-start | bytes 2654208 | tf_op jit(solution)/shard_map/reduce_scatter | solution.py:315
  439.3 8.0 copy-start.12
  483.4 12.7 copy-start.43
  483.4 12.7 copy-start.45
  483.4 12.7 copy-start.5
  508.4 328.0 %reduce-scatter.18.cloned.1.call-start = ((), (), s32[]{:S(2)}) async-start(), calls=%async_computation.15 | async-start | bytes 7962624 | tf_op jit(solution)/shard_map/reduce_scatter | solution.py:314
  516.6 11.8 copy-start.13
  580.6 9.8 copy-start.3
  602.1 11.4 copy-start.13
  665.1 9.8 copy-start.3
  710.4 218.5 %reduce-scatter.26.cloned.1.call-start = ((), (), s32[]{:S(2)}) async-start(), calls=%async_computation.19 | async-start | bytes 442368
  713.5 251.8 %reduce-scatter.24.cloned.1.call-start = ((), (), s32[]{:S(2)}) async-start(), calls=%async_computation.18 | async-start | bytes 442368
  715.0 315.5 %reduce-scatter.22.cloned.1.call-start = ((), (), s32[]{:S(2)}) async-start(), calls=%async_computation.17 | async-start | bytes 442368
  716.4 435.3 %reduce-scatter.16.cloned.1.call-start = ((), (), s32[]{:S(2)}) async-start(), calls=%async_computation.14 | async-start | bytes 7077888 | tf_op jit(solution)/shard_map/reduce_scatter | solution.py:331
  725.5 465.7 %all-reduce.14.cloned.1.call-start = ((), (), s32[]{:S(2)}) async-start(), calls=%async_computation.20 | async-start | bytes 2359296 | tf_op jit(solution)/shard_map/psum | solution.py:310
  836.5 566.4 %reduce-scatter.14.cloned.1.call-start = ((), (), s32[]{:S(2)}) async-start(), calls=%async_computation.13 | async-start | bytes 14155776 | tf_op jit(solution)/shard_map/reduce_scatter | solution.py:330
  849.9 41.2 %copy-start.25 = (bf16[1024,768]{1,0:T(8,128)(2,1)S(1)}, bf16[1024,768]{1,0:T(8,128)(2,1)}, u32[]{:S(2)}) copy-start(bf16[1024,768]{1,0:T(8,128)(2,1)} %param.19) | copy-start | bytes 4718596
  891.0 9.7 copy-start.57
  891.0 31.3 %copy-start.59 = (bf16[8,8]{1,0:T(8,128)(2,1)S(1)}, bf16[8,8]{1,0:T(8,128)(2,1)}, u32[]{:S(2)}) copy-start(bf16[8,8]{1,0:T(8,128)(2,1)} %param.30) | copy-start | bytes 388
  923.0 483.6 %copy-start.1 = (bf16[1,2048,768]{2,1,0:T(8,128)(2,1)S(1)}, bf16[1,2048,768]{2,1,0:T(8,128)(2,1)}, u32[]{:S(2)}) copy-start(bf16[1,2048,768]{2,1,0:T(8,128)(2,1)} %param.32) | copy-start | bytes 9437188
  (39 other events, 111.2 us)
Sparse Core Ops, SparseCore 0:
  10.2 67.8 all-gather.5
  80.3 39.9 all-gather.7
  508.5 65.6 reduce-scatter.19
  710.6 125.8 reduce-scatter.17
  839.5 61.4 reduce-scatter.25
  904.1 61.1 reduce-scatter.23
  969.2 61.2 reduce-scatter.21
  1034.7 117.0 reduce-scatter.15
  1154.3 36.8 all-reduce.13
  1195.2 207.5 reduce-scatter.13
where the time goes:
time: 1420 us; the launch traced here: 1410 us
  waiting for transfers between devices  598 us (42%)
  matrix products  287 us (20%)
  other arithmetic  182 us (13%)
  blocking collectives  153 us (11%)
  local copies, waits for them, and re-layouts  148 us (10%)
  starting transfers between devices  18.2 us (1%)
  between operations  16.7 us (1%)
    reduce_scatter x1, waiting for transfers between devices, per_device(): lax.psum_scatter(grad_w_in, 'dp', scatter_dimension=1, tiled=True)  212 us
    reduce_scatter x1, waiting for transfers between devices, per_device(): lax.psum_scatter(grad_w_out, 'dp', scatter_dimension=1, tiled=True)  114 us
    reduce_scatter x1, waiting for transfers between devices, per_device(): lax.psum_scatter(summed[0], 'dp', scatter_dimension=0, tiled=True)  111 us
    unnamed x13, waiting for transfers between devices  101 us
    dot_general x4, matrix products, masked_scores(): jnp.einsum('qhd,khd->hqk', q_block, key_rows, preferred_element_type=jnp....  50.5 us
    convert_element_type x2, other arithmetic, backward_block(): score_grad = (prob_rows * (prob_grad - row_delta)).astype(jnp.bfloat16)  43.4 us
    unnamed x152, local copies, waits for them, and re-layouts  42.2 us
    unnamed x2, blocking collectives  39.7 us
  transfers between devices with their start and end apart: 14, of which 9 were waited for; matrix products, arithmetic and copies ran while one was open for 32% of the time, Pallas kernels for 0%

commit v1 on v0

--- a/solution.py
+++ b/solution.py
@@ -64,15 +64,23 @@
     w_out,
     cotangent,
 ):
-    wqkv_full, wo_full, router_full, cgate_full, cvec_full, gain_attn, gain_ffn = (
-        lax.all_gather(wqkv, "dp", axis=0, tiled=True),
-        lax.all_gather(wo, "dp", axis=0, tiled=True),
-        lax.all_gather(router, "dp", axis=0, tiled=True),
-        lax.all_gather(const_gate, "dp", axis=0, tiled=True),
-        lax.all_gather(const_vec, "dp", axis=0, tiled=True),
-        lax.all_gather(gain1, "dp", axis=0, tiled=True),
-        lax.all_gather(gain2, "dp", axis=0, tiled=True),
-    )
+    kinds_in = router.shape[1]
+    small = jnp.concatenate(
+        [router, const_gate, const_vec, gain1[:, None], gain2[:, None]], axis=1
+    )
+    packed = jnp.concatenate(
+        [wqkv, wo, jnp.pad(small, ((0, 0), (0, 128 - small.shape[1])))], axis=1
+    )
+    whole = lax.all_gather(packed, "dp", axis=0, tiled=True)
+    qkv_cols = wqkv.shape[1]
+    wqkv_full = whole[:, :qkv_cols]
+    wo_full = whole[:, qkv_cols : qkv_cols + wo.shape[1]]
+    small_full = whole[:, qkv_cols + wo.shape[1] :]
+    router_full = small_full[:, :kinds_in]
+    cgate_full = small_full[:, kinds_in : kinds_in + 4]
+    cvec_full = small_full[:, kinds_in + 4 : kinds_in + 6]
+    gain_attn = small_full[:, kinds_in + 6]
+    gain_ffn = small_full[:, kinds_in + 7]
     tok_count, model_width = tokens.shape
     seq_count, seq_len = segments.shape
     head_count = HEADS
@@ -307,31 +315,35 @@
     attn_in_grad = jnp.einsum("tf,df->td", qkv_grad, wqkv_full, preferred_element_type=jnp.float32)
     grad_gain1 = jnp.sum(attn_in_grad * normed_one, axis=0)
     grad_tokens = mid_grad + norm_back(attn_in_grad * gain_one, normed_one, inverse_one)
-    summed = lax.psum(
-        (grad_wqkv, grad_wo, grad_router, grad_cgate, grad_cvec, grad_gain1, grad_gain2), "expert"
-    )
-    shares = (
-        lax.psum_scatter(summed[0], "dp", scatter_dimension=0, tiled=True),
-        lax.psum_scatter(summed[1], "dp", scatter_dimension=0, tiled=True),
-        lax.psum_scatter(summed[2], "dp", scatter_dimension=0, tiled=True),
-        lax.psum_scatter(summed[3], "dp", scatter_dimension=0, tiled=True),
-        lax.psum_scatter(summed[4], "dp", scatter_dimension=0, tiled=True),
-        lax.psum_scatter(summed[5], "dp", scatter_dimension=0, tiled=True),
-        lax.psum_scatter(summed[6], "dp", scatter_dimension=0, tiled=True),
-    )
-    grad_gate_mix = lax.psum(grad_mix, ("dp", "expert"))
+    grad_w_out = jnp.einsum(
+        "erf,erd->efd", hidden_act, grad_sent, preferred_element_type=jnp.float32
+    ).astype(jnp.bfloat16)
     grad_w_in = jnp.einsum(
         "erd,erf->edf", recv_rows, front_grad, preferred_element_type=jnp.float32
-    )
-    grad_w_out = jnp.einsum(
-        "erf,erd->efd", hidden_act, grad_sent, preferred_element_type=jnp.float32
-    )
-    expert_shares = (
-        lax.psum_scatter(grad_w_in, "dp", scatter_dimension=1, tiled=True),
-        lax.psum_scatter(grad_w_out, "dp", scatter_dimension=1, tiled=True),
-    )
-    in_share = expert_shares[0]
-    out_share = expert_shares[1]
+    ).astype(jnp.bfloat16)
+    out_share = lax.psum_scatter(grad_w_out, "dp", scatter_dimension=1, tiled=True).astype(
+        jnp.float32
+    )
+    in_share = lax.psum_scatter(grad_w_in, "dp", scatter_dimension=1, tiled=True).astype(
+        jnp.float32
+    )
+    large = jnp.concatenate([grad_wqkv, grad_wo], axis=1).astype(jnp.bfloat16)
+    large_share = lax.psum_scatter(large, "dp", scatter_dimension=0, tiled=True)
+    minor = jnp.concatenate(
+        [grad_router, grad_cgate, grad_cvec, grad_gain1[:, None], grad_gain2[:, None]], axis=1
+    )
+    minor_share = lax.psum_scatter(minor, "dp", scatter_dimension=0, tiled=True)
+    summed = lax.psum((large_share.astype(jnp.float32), minor_share), "expert")
+    grad_gate_mix = lax.psum(grad_mix, ("dp", "expert"))
+    shares = (
+        summed[0][:, : wqkv.shape[1]],
+        summed[0][:, wqkv.shape[1] :],
+        summed[1][:, :kinds_in],
+        summed[1][:, kinds_in : kinds_in + 4],
+        summed[1][:, kinds_in + 4 : kinds_in + 6],
+        summed[1][:, kinds_in + 6],
+        summed[1][:, kinds_in + 7],
+    )
     return (
         mixed,
         grad_tokens,

time: 1420 us -> 1030 us (0.73)
  waiting for transfers between devices: 598 us -> 303 us
  blocking collectives: 153 us -> 66.8 us
    reduce_scatter x1, waiting for transfers between devices: 212 us -> 87.1 us  [per_device(): lax.psum_scatter(grad_w_in, 'dp', scatter_dimension=1, tiled=True)]
    unnamed x13 -> x6, waiting for transfers between devices: 101 us -> 0.08 us
    all_gather x3 -> x0, blocking collectives: 67.8 us -> none  [the longest x1 26.3 us: per_device(): lax.all_gather(router, 'dp', axis=0, tiled=True)]
    reduce_scatter x1, waiting for transfers between devices: 114 us -> 54.7 us  [per_device(): lax.psum_scatter(grad_w_out, 'dp', scatter_dimension=1, tiled=True)]
    all_gather x2 -> x1, waiting for transfers between devices: 0.01 us -> 39.9 us  [per_device(): whole = lax.all_gather(packed, 'dp', axis=0, tiled=True)]
    unnamed x2 -> x0, blocking collectives: 39.7 us -> none
    psum x1 -> x0, waiting for transfers between devices: 39.4 us -> none  [per_device(): lax.psum((grad_wqkv, grad_wo, grad_router, grad_cgate, grad_cvec, grad_ga...]
    psum x1, blocking collectives: 6.33 us -> 27.9 us  [per_device(): summed = lax.psum((large_share.astype(jnp.float32), minor_share), 'expert')]
  transfers between devices with their start and end apart: 14 -> 9, of which waited for: 9 -> 7; matrix products, arithmetic and copies ran while one was open for 32% -> 15% of each run, Pallas kernels for 0% -> 0%
where the time goes in v1:
time: 1030 us
  waiting for transfers between devices  303 us (29%)
  matrix products  279 us (27%)
  other arithmetic  189 us (18%)
  local copies, waits for them, and re-layouts  146 us (14%)
  blocking collectives  66.8 us (6%)
  starting transfers between devices  17.8 us (2%)
  between operations  15 us (1%)
    reduce_scatter x1, waiting for transfers between devices, per_device(): large_share = lax.psum_scatter(large, 'dp', scatter_dimension=0, tiled=True)  96.4 us
    reduce_scatter x1, waiting for transfers between devices, per_device(): lax.psum_scatter(grad_w_in, 'dp', scatter_dimension=1, tiled=True)  87.1 us
    reduce_scatter x1, waiting for transfers between devices, per_device(): lax.psum_scatter(grad_w_out, 'dp', scatter_dimension=1, tiled=True)  54.7 us
    dot_general x4, matrix products, masked_scores(): jnp.einsum('qhd,khd->hqk', q_block, key_rows, preferred_element_type=jnp....  50.2 us
    convert_element_type x2, other arithmetic, backward_block(): score_grad = (prob_rows * (prob_grad - row_delta)).astype(jnp.bfloat16)  43.2 us
    all_gather x1, waiting for transfers between devices, per_device(): whole = lax.all_gather(packed, 'dp', axis=0, tiled=True)  39.9 us
    psum x1, blocking collectives, per_device(): grad_gate_mix = lax.psum(grad_mix, ('dp', 'expert'))  38.9 us
    dot_general x2, matrix products, backward_block(): jnp.einsum('qhd,khd->hqk', out_grad_block, value_seqs[seq_index], preferr...  34.8 us
  transfers between devices with their start and end apart: 9, of which 7 were waited for; matrix products, arithmetic and copies ran while one was open for 15% of the time, Pallas kernels for 0%

profile of v1, /device:TPU:0, one launch (start us, length us, event | category | flops | bytes accessed | tf_op | source)
XLA Modules:
  0.0 1026.5 jit_solution(812680198165655639)
XLA Ops:
  33.1 8.5 mul.725
  41.8 8.4 scatter_custom_fusion
  55.7 39.9 %all-gather.2.cloned.1.call-done = bf16[768,3200]{1,0:T(8,128)(2,1)} async-done(((bf16[96,3200]{1,0:T(8,128)(2,1)}), bf16[768,3200]{1,0:T(8,128)(2,1)}) %all-gather.2.cloned.1.call-update) | async-done | bytes 4915216 | tf_op jit(solution)/shard_map/all_gather | solution.py:74
  97.6 6.6 fusion.77
  110.7 82.9 %while.32 = (s32[]{:T(128)}, bf16[2,512,12,64]{1,3,2,0:T(8,128)(2,1)}, f32[2,12,512,1]{2,1,3,0:T(8,128)S(1)}, s32[2]{0:T(128)S(1)}, s32[1,1024]{1,0:T(1,128)S(1)...) while((s32[]{:T(128)}, ...), condition=%wide.region_4.5_spmd.clone, body=%wide.region_1.4_spmd.sunk.clone | while | flops 1668803072 | bytes 102226280 | solution.py:137
  114.3 13.6 %select_reduce_fusion.8 = (f32[12,512]{1,0:T(8,128)S(1)}, f32[12,512,1024]{2,1,0:T(8,128)}) fusion(pred[512,1024]{1,0:T(8,128)(4,1)S(1)} %fusion.210, bf16[1,1024,12,64]{1,3,2,0:T(8,128)(2,1)} %get-tuple-element.646, bf16[1,1024,12,64]{1,3,2,0:T(8,128)(2,1)} %get-tuple-element.645, s32[]{:T(128)S(6)} %select_n.232), kind=kOutput, calls=%fused_computation.7.clone.1.clone | convolution fusion | flops 817883136 | bytes 28073988 | tf_op jit(solution)/shard_map/while/body/eval_jaxpr/qhd,khd->hqk/dot_general | solution.py:43
  128.0 11.6 %fusion.211 = f32[12,512]{1,0:T(8,128)S(1)} fusion(f32[12,512,1024]{2,1,0:T(8,128)} %get-tuple-element.579, f32[12,512]{1,0:T(8,128)S(1)} %get-tuple-element.580, pred[512,1024]{1,0:T(8,128)(4,1)S(1)} %fusion.210), kind=kLoop, calls=%fused_computation.8.clone.1.clone | loop fusion | flops 18868224 | bytes 25739264 | tf_op jit(solution)/shard_map/while/body/eval_jaxpr/reduce_sum | solution.py:130
  139.6 11.6 %bitcast_dynamic-update-slice_fusion.15 = bf16[2,512,12,64]{1,3,2,0:T(8,128)(2,1)S(1)} fusion(bf16[2,512,12,64]{1,3,2,0:T(8,128)(2,1)S(1)} %copy-done.20, s32[]{:T(128)S(6)} %copy.156, bf16[1,1024,12,64]{1,3,2,0:T(8,128)(2,1)S(1)} %copy-done.8, f32[12,512,1024]{2,1,0:T(8,128)} %get-tuple-element.579, f32[12,512]{1,0:T(8,128)S(1)} %fusion.211, ...), kind=kOutput, calls=%fused_computation.12.clone.1.clone | convolution fusion | flops 830472192 | bytes 28901380 | tf_op jit(solution)/shard_map/while/body/eval_jaxpr/hqk,khd->qhd/dot_general | solution.py:132
  155.4 13.6 %select_reduce_fusion.8 = (f32[12,512]{1,0:T(8,128)S(1)}, f32[12,512,1024]{2,1,0:T(8,128)}) fusion(pred[512,1024]{1,0:T(8,128)(4,1)S(1)} %fusion.210, bf16[1,1024,12,64]{1,3,2,0:T(8,128)(2,1)} %get-tuple-element.646, bf16[1,1024,12,64]{1,3,2,0:T(8,128)(2,1)} %get-tuple-element.645, s32[]{:T(128)S(6)} %select_n.232), kind=kOutput, calls=%fused_computation.7.clone.1.clone | convolution fusion | flops 817883136 | bytes 28073988 | tf_op jit(solution)/shard_map/while/body/eval_jaxpr/qhd,khd->hqk/dot_general | solution.py:43
  169.1 11.6 %fusion.211 = f32[12,512]{1,0:T(8,128)S(1)} fusion(f32[12,512,1024]{2,1,0:T(8,128)} %get-tuple-element.579, f32[12,512]{1,0:T(8,128)S(1)} %get-tuple-element.580, pred[512,1024]{1,0:T(8,128)(4,1)S(1)} %fusion.210), kind=kLoop, calls=%fused_computation.8.clone.1.clone | loop fusion | flops 18868224 | bytes 25739264 | tf_op jit(solution)/shard_map/while/body/eval_jaxpr/reduce_sum | solution.py:130
  180.7 11.6 %bitcast_dynamic-update-slice_fusion.15 = bf16[2,512,12,64]{1,3,2,0:T(8,128)(2,1)S(1)} fusion(bf16[2,512,12,64]{1,3,2,0:T(8,128)(2,1)S(1)} %copy-done.20, s32[]{:T(128)S(6)} %copy.156, bf16[1,1024,12,64]{1,3,2,0:T(8,128)(2,1)S(1)} %copy-done.8, f32[12,512,1024]{2,1,0:T(8,128)} %get-tuple-element.579, f32[12,512]{1,0:T(8,128)S(1)} %fusion.211, ...), kind=kOutput, calls=%fused_computation.12.clone.1.clone | convolution fusion | flops 830472192 | bytes 28901380 | tf_op jit(solution)/shard_map/while/body/eval_jaxpr/hqk,khd->qhd/dot_general | solution.py:132
  210.8 7.2 gather_fusion
  227.5 7.9 gather_fusion.2
  246.8 12.4 %convolution_bitcast_fusion = f32[1,1024,4096]{2,1,0:T(8,128)} fusion(bf16[1024,768]{1,0:T(8,128)(2,1)} %bitcast.37, bf16[1,768,4096]{2,1,0:T(8,128)(2,1)} %param.31), kind=kOutput, calls=%fused_computation.58 | convolution fusion | flops 6442450944 | bytes 24641536 | tf_op jit(solution)/shard_map/erd,edf->erf/dot_general | solution.py:173
  259.3 7.7 all-to-all-done.2
  266.9 12.3 %fusion.60 = (bf16[1024,2048]{1,0:T(8,128)(2,1)S(1)}, bf16[1024,2048]{1,0:T(8,128)(2,1)S(1)}, bf16[1,1024,2048]{2,1,0:T(8,128)(2,1)}) fusion(f32[1,1024,4096]{2,1,0:T(8,128)} %convolution_bitcast_fusion, bf16[1024,768]{1,0:T(8,128)(2,1)} %bitcast.49, bf16[1,2048,768]{2,1,0:T(8,128)(2,1)S(1)} %copy-done), kind=kOutput, calls=%fused_computation.93 | convolution fusion | flops 3254779904 | bytes 34078720 | tf_op jit(solution)/shard_map/erd,efd->erf/dot_general | solution.py:211
  279.3 12.4 %fusion.96 = bf16[1,1024,768]{2,1,0:T(8,128)(2,1)S(1)} fusion(bf16[1,768,4096]{2,1,0:T(8,128)(2,1)} %param.31, bf16[1024,2048]{1,0:T(8,128)(2,1)S(1)} %get-tuple-element.395, bf16[1024,2048]{1,0:T(8,128)(2,1)S(1)} %get-tuple-element.394), kind=kOutput, calls=%fused_computation.146 | convolution fusion | flops 6460014592 | bytes 16252928 | tf_op jit(solution)/shard_map/erf,edf->erd/dot_general | solution.py:215
  296.3 12.6 %reduce.19 = bf16[1024,768]{1,0:T(8,128)(2,1)} reduce(bf16[1024,1,768]{2,1,0:T(2,128)(2,1)} %bitcast.321, bf16[]{:T(256)} %broadcast.527), dimensions={1}, to_apply=%bitcast.244.reduce_sub_computation | reduce | bytes 3145730
  319.2 5.6 fusion.91
  327.3 11.8 %reduce.18 = bf16[1024,768]{1,0:T(8,128)(2,1)} reduce(bf16[1024,1,768]{2,1,0:T(2,128)(2,1)S(1)} %bitcast.322, bf16[]{:T(256)} %broadcast.527), dimensions={1}, to_apply=%bitcast.245.reduce_sub_computation | reduce | bytes 3145730
  354.0 13.4 %all-to-all-done.1 = bf16[4,2,98304]{2,1,0:T(2,128)(2,1)} async-done(((bf16[4,2,98304]{2,1,0:T(2,128)(2,1)}), bf16[4,2,98304]{2,1,0:T(2,128)(2,1)}, u32[]{:S(2)}, u32[]{:S(2)}) %all-to-all-start.1) | async-done | bytes 1572896 | tf_op jit(solution)/shard_map/all_to_all | solution.py:181
  375.4 9.4 gather_fusion.3
  384.8 10.1 gather_fusion.1
  399.6 27.0 %multiply_reduce_fusion.1 = (f32[1024,2]{1,0:T(8,128)S(1)}, f32[1024,768]{1,0:T(8,128)}) fusion(f32[1024,768]{1,0:T(8,128)} %convert_element_type.292, f32[1024,2]{1,0:T(8,128)} %copy.112, f32[1024,2]{1,0:T(8,128)} %copy.121, f32[1024,768]{1,0:T(8,128)} %get-tuple-element.410, f32[1024,2]{1,0:T(8,128)} %copy.120, f32[1024,768]{1,0:T(8,128)} %get-tuple-element.409, ...), kind=kLoop, calls=%fused_computation.73 | loop fusion | flops 16513024 | bytes 22069248 | tf_op jit(solution)/shard_map/reduce_sum | solution.py:202
  427.9 8.0 reshape.792
  436.9 12.0 %reduce_sum.257 = f32[1024,768]{1,0:T(8,128)} reduce(f32[1024,2,768]{2,1,0:T(2,128)} %reshape.792, f32[]{:T(128)} %constant.203.clone.1), dimensions={1}, to_apply=%region_18.19 | reduce | flops 786432 | bytes 9437188 | tf_op jit(solution)/shard_map/reduce_sum | solution.py:226
  462.8 169.6 %while.33 = (s32[]{:T(128)}, f32[2,512,12,64]{1,3,2,0:T(8,128)}, f32[2,1024,12,64]{1,3,2,0:T(8,128)}, f32[2,1024,12,64]{1,3,2,0:T(8,128)}, s32[2]{0:T(128)S(1)},...) while((s32[]{:T(128)}, f32[2,512,12,64]{1,3,2,0:T(8,128)}, ...), condition=%wide.region_31.32_spmd.clone, body=%wide.region_29.31_spmd.sunk.clone | while | flops 4103596544 | bytes 219347312 | solution.py:297
  466.1 11.4 %fusion.220 = f32[12,512,1024]{2,1,0:T(8,128)} fusion(bf16[1,1024,12,64]{1,3,2,0:T(8,128)(2,1)S(1)} %get-tuple-element.677, bf16[1,1024,12,64]{1,3,2,0:T(8,128)(2,1)} %get-tuple-element.676, s32[]{:T(128)S(6)} %select_n.237), kind=kOutput, calls=%fused_computation.40.clone.1.clone | convolution fusion | flops 805306368 | bytes 27525124 | tf_op jit(solution)/shard_map/while/body/eval_jaxpr/qhd,khd->hqk/dot_general | solution.py:43
  477.5 12.7 %bitcast_dynamic-update-slice_fusion.19 = f32[2,1024,12,64]{1,3,2,0:T(8,128)} fusion(f32[2,1024,12,64]{1,3,2,0:T(8,128)} %get-tuple-element.662, s32[]{:T(128)S(6)} %copy.166, f32[12,512,1024]{2,1,0:T(8,128)} %fusion.220, f32[12,512]{1,0:T(8,128)S(1)} %dynamic-slice_bitcast_fusion.3, pred[512,1024]{1,0:T(8,128)(4,1)S(1)} %fusion.221, ...), kind=kOutput, calls=%fused_computation.31.clone.1.clone | convolution fusion | flops 824180736 | bytes 29655048 | tf_op jit(solution)/shard_map/while/body/eval_jaxpr/hqk,qhd->khd/dot_general | solution.py:289
  490.2 17.4 %multiply_reduce_fusion.12 = (f32[12,512]{1,0:T(8,128)S(1)}, f32[12,512,1024]{2,1,0:T(8,128)}) fusion(f32[12,512,1024]{2,1,0:T(8,128)} %fusion.220, f32[12,512]{1,0:T(8,128)S(1)} %dynamic-slice_bitcast_fusion.3, pred[512,1024]{1,0:T(8,128)(4,1)S(1)} %fusion.221, bf16[1,1024,12,64]{1,3,2,0:T(8,128)(2,1)} %get-tuple-element.680, ...), kind=kOutput, calls=%fused_computation.24.clone.1.clone | convolution fusion | flops 830466048 | bytes 53264388 | tf_op jit(solution)/shard_map/while/body/eval_jaxpr/qhd,khd->hqk/dot_general | solution.py:275
  507.6 21.6 %multiply_convert_fusion.7 = bf16[12,512,1024]{2,1,0:T(8,128)(2,1)} fusion(f32[12,512,1024]{2,1,0:T(8,128)} %get-tuple-element.606, f32[12,512,1024]{2,1,0:T(8,128)} %fusion.220, f32[12,512]{1,0:T(8,128)S(1)} %get-tuple-element.607, f32[12,512]{1,0:T(8,128)S(1)} %dynamic-slice_bitcast_fusion.3, pred[512,1024]{1,0:T(8,128)(4,1)S(1)} %fusion.221), kind=kLoop, calls=%fused_computation.23.clone.1.clone | loop fusion | flops 31457280 | bytes 63488000 | tf_op jit(solution)/shard_map/while/body/eval_jaxpr/convert_element_type | solution.py:282
  529.2 9.8 bitcast_dynamic-update-slice_fusion.17
  539.0 8.5 bitcast_dynamic-update-slice_fusion.18
  550.6 11.4 %fusion.220 = f32[12,512,1024]{2,1,0:T(8,128)} fusion(bf16[1,1024,12,64]{1,3,2,0:T(8,128)(2,1)S(1)} %get-tuple-element.677, bf16[1,1024,12,64]{1,3,2,0:T(8,128)(2,1)} %get-tuple-element.676, s32[]{:T(128)S(6)} %select_n.237), kind=kOutput, calls=%fused_computation.40.clone.1.clone | convolution fusion | flops 805306368 | bytes 27525124 | tf_op jit(solution)/shard_map/while/body/eval_jaxpr/qhd,khd->hqk/dot_general | solution.py:43
  562.1 12.6 %bitcast_dynamic-update-slice_fusion.19 = f32[2,1024,12,64]{1,3,2,0:T(8,128)} fusion(f32[2,1024,12,64]{1,3,2,0:T(8,128)} %get-tuple-element.662, s32[]{:T(128)S(6)} %copy.166, f32[12,512,1024]{2,1,0:T(8,128)} %fusion.220, f32[12,512]{1,0:T(8,128)S(1)} %dynamic-slice_bitcast_fusion.3, pred[512,1024]{1,0:T(8,128)(4,1)S(1)} %fusion.221, ...), kind=kOutput, calls=%fused_computation.31.clone.1.clone | convolution fusion | flops 824180736 | bytes 29655048 | tf_op jit(solution)/shard_map/while/body/eval_jaxpr/hqk,qhd->khd/dot_general | solution.py:289
  574.6 17.4 %multiply_reduce_fusion.12 = (f32[12,512]{1,0:T(8,128)S(1)}, f32[12,512,1024]{2,1,0:T(8,128)}) fusion(f32[12,512,1024]{2,1,0:T(8,128)} %fusion.220, f32[12,512]{1,0:T(8,128)S(1)} %dynamic-slice_bitcast_fusion.3, pred[512,1024]{1,0:T(8,128)(4,1)S(1)} %fusion.221, bf16[1,1024,12,64]{1,3,2,0:T(8,128)(2,1)} %get-tuple-element.680, ...), kind=kOutput, calls=%fused_computation.24.clone.1.clone | convolution fusion | flops 830466048 | bytes 53264388 | tf_op jit(solution)/shard_map/while/body/eval_jaxpr/qhd,khd->hqk/dot_general | solution.py:275
  592.0 21.6 %multiply_convert_fusion.7 = bf16[12,512,1024]{2,1,0:T(8,128)(2,1)} fusion(f32[12,512,1024]{2,1,0:T(8,128)} %get-tuple-element.606, f32[12,512,1024]{2,1,0:T(8,128)} %fusion.220, f32[12,512]{1,0:T(8,128)S(1)} %get-tuple-element.607, f32[12,512]{1,0:T(8,128)S(1)} %dynamic-slice_bitcast_fusion.3, pred[512,1024]{1,0:T(8,128)(4,1)S(1)} %fusion.221), kind=kLoop, calls=%fused_computation.23.clone.1.clone | loop fusion | flops 31457280 | bytes 63488000 | tf_op jit(solution)/shard_map/while/body/eval_jaxpr/convert_element_type | solution.py:282
  613.6 9.8 bitcast_dynamic-update-slice_fusion.17
  623.4 8.6 bitcast_dynamic-update-slice_fusion.18
  652.8 6.4 fusion.69
  661.2 7.8 fusion.79
  673.9 6.9 convolution_convert_fusion.1
  683.7 12.4 %fusion.50 = bf16[1,768,4096]{2,1,0:T(8,128)(2,1)} fusion(bf16[1024,768]{1,0:T(8,128)(2,1)} %bitcast.37, bf16[1024,2048]{1,0:T(8,128)(2,1)} %copy-done.54, bf16[1024,2048]{1,0:T(8,128)(2,1)} %copy-done.53), kind=kOutput, calls=%fused_computation.77 | convolution fusion | flops 6462373888 | bytes 16252928 | tf_op jit(solution)/shard_map/erd,erf->edf/dot_general | solution.py:321
  697.1 38.9 %psum.23 = f32[8,8]{0,1:T(8,128)S(1)} all-reduce(f32[8,8]{0,1:T(8,128)S(1)} %convolution_bitcast_fusion.3), channel_id=1, replica_groups=mesh['dp'=8,'expert'=4] {'dp','expert'}, use_global_device_ids=true, to_apply=%region_41.42 | all-reduce | flops 64 | bytes 512 | tf_op jit(solution)/shard_map/psum | solution.py:337
  743.2 54.7 %reduce-scatter.11.cloned.1.call-done = bf16[1,256,768]{2,1,0:T(8,128)(2,1)} async-done(((bf16[1,2048,768]{2,1,0:T(8,128)(2,1)}), bf16[1,256,768]{2,1,0:T(8,128)(2,1)}) %reduce-scatter.11.cloned.1.call-update) | async-done | bytes 393232 | tf_op jit(solution)/shard_map/reduce_scatter | solution.py:324
  799.9 96.4 %reduce-scatter.7.cloned.1.call-done = bf16[96,3072]{1,0:T(8,128)(2,1)} async-done(((bf16[768,3072]{1,0:T(8,128)(2,1)}), bf16[96,3072]{1,0:T(8,128)(2,1)}) %reduce-scatter.7.cloned.1.call-update) | async-done | bytes 589840 | tf_op jit(solution)/shard_map/reduce_scatter | solution.py:331
  896.2 27.9 %all-reduce.7 = (f32[96,3072]{1,0:T(8,128)}, f32[96,16]{0,1:T(8,128)S(1)}) all-reduce(bf16[96,3072]{1,0:T(8,128)(2,1)} %reduce-scatter.7.cloned.1.call-done, f32[96,16]{0,1:T(8,128)S(1)} %copy.132), channel_id=1, replica_groups=mesh['dp'=8,'expert'=4] {'expert'}, use_global_device_ids=true, to_apply=%region_36.37 | all-reduce | flops 296448 | bytes 1781760 | tf_op jit(solution)/shard_map/psum | solution.py:336
  930.2 87.1 %reduce-scatter.9.cloned.1.call-done = bf16[1,96,4096]{2,1,0:T(8,128)(2,1)} async-done(((bf16[1,768,4096]{2,1,0:T(8,128)(2,1)}), bf16[1,96,4096]{2,1,0:T(8,128)(2,1)}) %reduce-scatter.9.cloned.1.call-update) | async-done | bytes 786448 | tf_op jit(solution)/shard_map/reduce_scatter | solution.py:327
  (290 shorter events, 194.0 us)
Async XLA Ops:
  7.2 259.8 %copy-start = (bf16[1,2048,768]{2,1,0:T(8,128)(2,1)S(1)}, bf16[1,2048,768]{2,1,0:T(8,128)(2,1)}, u32[]{:S(2)}) copy-start(bf16[1,2048,768]{2,1,0:T(8,128)(2,1)} %param.32) | copy-start | bytes 9437188
  7.2 8.2 copy-start.34
  7.2 88.4 %all-gather.2.cloned.1.call-start = ((), (), s32[]{:S(2)}) async-start(), calls=%async_computation.8 | async-start | bytes 5529600 | tf_op jit(solution)/shard_map/all_gather | solution.py:74
  25.3 3.4 copy-start.4
  53.3 50.9 %copy-start.46 = (f32[1024]{0:T(1024)}, f32[1024]{0:T(1024)S(1)}, u32[]{:S(2)}) copy-start(f32[1024]{0:T(1024)S(1)} %add_rsqrt_fusion.1) | copy-start | bytes 12292
  55.7 51.0 %copy-start.28 = (f32[1024,32]{0,1:T(8,128)}, f32[1024,32]{0,1:T(8,128)S(1)}, u32[]{:S(2)}) copy-start(f32[1024,32]{0,1:T(8,128)S(1)} %get-tuple-element.435) | copy-start | bytes 393220
  97.6 6.6 copy-start.42
  128.0 11.6 %copy-start.8 = (bf16[1,1024,12,64]{1,3,2,0:T(8,128)(2,1)S(1)}, bf16[1,1024,12,64]{1,3,2,0:T(8,128)(2,1)}, u32[]{:S(2)}) copy-start(bf16[1,1024,12,64]{1,3,2,0:T(8,128)(2,1)} %get-tuple-element.647) | copy-start | bytes 4718596 | tf_op jit(solution)/shard_map/while
  128.0 11.7 %copy-start.20 = (bf16[2,512,12,64]{1,3,2,0:T(8,128)(2,1)S(1)}, bf16[2,512,12,64]{1,3,2,0:T(8,128)(2,1)}, u32[]{:S(2)}) copy-start(bf16[2,512,12,64]{1,3,2,0:T(8,128)(2,1)} %get-tuple-element.633) | copy-start | bytes 4718596 | tf_op jit(solution)/shard_map/while
  169.1 11.6 %copy-start.8 = (bf16[1,1024,12,64]{1,3,2,0:T(8,128)(2,1)S(1)}, bf16[1,1024,12,64]{1,3,2,0:T(8,128)(2,1)}, u32[]{:S(2)}) copy-start(bf16[1,1024,12,64]{1,3,2,0:T(8,128)(2,1)} %get-tuple-element.647) | copy-start | bytes 4718596 | tf_op jit(solution)/shard_map/while
  169.1 11.7 %copy-start.20 = (bf16[2,512,12,64]{1,3,2,0:T(8,128)(2,1)S(1)}, bf16[2,512,12,64]{1,3,2,0:T(8,128)(2,1)}, u32[]{:S(2)}) copy-start(bf16[2,512,12,64]{1,3,2,0:T(8,128)(2,1)} %get-tuple-element.633) | copy-start | bytes 4718596 | tf_op jit(solution)/shard_map/while
  193.6 3.6 copy-start.23
  197.2 3.5 copy-start.27
  197.2 3.6 copy-start.5
  197.2 3.6 copy-start.40
  202.4 3.3 copy-start.35
  203.9 7.0 copy-start.49
  218.0 24.5 %all-to-all-start = ((bf16[4,256,768]{2,1,0:T(8,128)(2,1)}), bf16[4,256,768]{2,1,0:T(8,128)(2,1)}, u32[]{:S(2)}, u32[]{:S(2)}) async-start(bf16[4,256,768]{2,1,0:T(8,128)(2,1)} %bitcast.332), calls=%async_computation | async-start | bytes 3145728 | tf_op jit(solution)/shard_map/all_to_all | solution.py:172
  242.5 24.5 %all-to-all-start.2 = ((bf16[4,256,768]{2,1,0:T(8,128)(2,1)}), bf16[4,256,768]{2,1,0:T(8,128)(2,1)}, u32[]{:S(2)}, u32[]{:S(2)}) async-start(bf16[4,256,768]{2,1,0:T(8,128)(2,1)} %bitcast.333), calls=%async_computation.2 | async-start | bytes 3145728 | tf_op jit(solution)/shard_map/all_to_all | solution.py:210
  279.3 12.4 %copy-start.53 = (bf16[1024,2048]{1,0:T(8,128)(2,1)}, bf16[1024,2048]{1,0:T(8,128)(2,1)S(1)}, u32[]{:S(2)}) copy-start(bf16[1024,2048]{1,0:T(8,128)(2,1)S(1)} %get-tuple-element.394) | copy-start | bytes 12582916
  279.3 12.4 %copy-start.54 = (bf16[1024,2048]{1,0:T(8,128)(2,1)}, bf16[1024,2048]{1,0:T(8,128)(2,1)S(1)}, u32[]{:S(2)}) copy-start(bf16[1024,2048]{1,0:T(8,128)(2,1)S(1)} %get-tuple-element.395) | copy-start | bytes 12582916
  312.6 30.4 %all-to-all-start.3 = ((bf16[4,2,98304]{2,1,0:T(2,128)(2,1)}), bf16[4,2,98304]{2,1,0:T(2,128)(2,1)}, u32[]{:S(2)}, u32[]{:S(2)}) async-start(bf16[4,2,98304]{2,1,0:T(2,128)(2,1)} %reshape.844), calls=%async_computation.3 | async-start | bytes 3145728 | tf_op jit(solution)/shard_map/all_to_all | solution.py:218
  339.1 8.4 copy-start.12
  343.0 24.5 %all-to-all-start.1 = ((bf16[4,2,98304]{2,1,0:T(2,128)(2,1)}), bf16[4,2,98304]{2,1,0:T(2,128)(2,1)}, u32[]{:S(2)}, u32[]{:S(2)}) async-start(bf16[4,2,98304]{2,1,0:T(2,128)(2,1)} %reshape.846), calls=%async_computation.1 | async-start | bytes 3145728 | tf_op jit(solution)/shard_map/all_to_all | solution.py:181
  347.3 394.9 %reduce-scatter.13.cloned.1.call-start = ((), (), s32[]{:S(2)}) async-start(), calls=%async_computation.12 | async-start | bytes 442368
  371.9 3.5 copy-start.39
  399.6 27.3 %copy-start.10 = (bf16[1024,768]{1,0:T(8,128)(2,1)S(1)}, bf16[1024,768]{1,0:T(8,128)(2,1)}, u32[]{:S(2)}) copy-start(bf16[1024,768]{1,0:T(8,128)(2,1)} %copy-done.9) | copy-start | bytes 4718596
  426.9 22.5 %copy-start.32 = (bf16[1024,8]{0,1:T(8,128)(2,1)}, bf16[1024,8]{0,1:T(8,128)(2,1)S(1)}, u32[]{:S(2)}) copy-start(bf16[1024,8]{0,1:T(8,128)(2,1)S(1)} %select_reduce_fusion.1) | copy-start | bytes 49156
  451.0 4.8 copy-start.15
  451.0 4.8 copy-start.16
  457.9 4.9 copy-start.18
  457.9 4.9 copy-start.2
  466.1 11.4 %copy-start.13 = (bf16[1,1024,12,64]{1,3,2,0:T(8,128)(2,1)S(1)}, bf16[1,1024,12,64]{1,3,2,0:T(8,128)(2,1)}, u32[]{:S(2)}) copy-start(bf16[1,1024,12,64]{1,3,2,0:T(8,128)(2,1)} %get-tuple-element.679) | copy-start | bytes 4718596 | tf_op jit(solution)/shard_map/while
  529.2 9.8 copy-start.3
  550.6 11.4 %copy-start.13 = (bf16[1,1024,12,64]{1,3,2,0:T(8,128)(2,1)S(1)}, bf16[1,1024,12,64]{1,3,2,0:T(8,128)(2,1)}, u32[]{:S(2)}) copy-start(bf16[1,1024,12,64]{1,3,2,0:T(8,128)(2,1)} %get-tuple-element.679) | copy-start | bytes 4718596 | tf_op jit(solution)/shard_map/while
  613.6 9.8 copy-start.3
  650.4 8.9 copy-start.26
  652.8 6.5 copy-start.7
  652.8 6.5 copy-start.44
  652.8 6.5 copy-start.45
  652.8 7.2 copy-start.38
  652.8 7.2 copy-start.41
  652.8 7.2 copy-start.50
  661.0 137.0 %reduce-scatter.11.cloned.1.call-start = ((), (), s32[]{:S(2)}) async-start(), calls=%async_computation.11 | async-start | bytes 3538944 | tf_op jit(solution)/shard_map/reduce_scatter | solution.py:324
  669.1 227.2 %reduce-scatter.7.cloned.1.call-start = ((), (), s32[]{:S(2)}) async-start(), calls=%async_computation.9 | async-start | bytes 5308416 | tf_op jit(solution)/shard_map/reduce_scatter | solution.py:331
  683.7 333.7 %reduce-scatter.9.cloned.1.call-start = ((), (), s32[]{:S(2)}) async-start(), calls=%async_computation.10 | async-start | bytes 7077888 | tf_op jit(solution)/shard_map/reduce_scatter | solution.py:327
  696.2 40.4 %copy-start.52 = (bf16[8,8]{1,0:T(8,128)(2,1)S(1)}, bf16[8,8]{1,0:T(8,128)(2,1)}, u32[]{:S(2)}) copy-start(bf16[8,8]{1,0:T(8,128)(2,1)} %param.30) | copy-start | bytes 388
  742.2 277.6 %copy-start.1 = (bf16[1,2048,768]{2,1,0:T(8,128)(2,1)S(1)}, bf16[1,2048,768]{2,1,0:T(8,128)(2,1)}, u32[]{:S(2)}) copy-start(bf16[1,2048,768]{2,1,0:T(8,128)(2,1)} %param.32) | copy-start | bytes 9437188
  (23 other events, 47.3 us)
Sparse Core Ops, SparseCore 0:
  11.1 84.4 all-gather.1
  661.1 59.5 reduce-scatter.12
  724.3 73.5 reduce-scatter.10
  801.4 94.7 reduce-scatter.6
  899.7 117.6 reduce-scatter.8
